TPU v7x, 256 devices: a whole 4x4x8 slice. The times are simulated.
256 devices in a mesh: term: 16 (over z, core), sector: 16 (over y, x).
Axes of the slice: x: 4, y: 4, z: 8, core: 2. Of those that a mesh axis runs over, the one named last changes fastest.
Arguments:
- wavefunction: bfloat16 [96, 256, 256], P('sector'), may hold values from -6 to 6
- left_env: bfloat16 [48, 96, 256, 256], P('term', 'sector')
- right_env: bfloat16 [48, 96, 256, 256], P('term', 'sector')
- source: int32 [48, 96], P('term'), may hold values from 0 to 95, as said below
- block_size: int32 [96, 2], P('sector'), may hold values from 32 to 256
Outputs:
- first_product: float32 [96, 256, 256], P('sector', 'term')
- second_product: float32 [96, 256, 256], P('sector', 'term')
Inputs may be any that keep to these rules, and one draw needn't show every extreme that they name: Owner of sector s is s // 6. Among the 3 x 6 entries of source in one device's rows (one index of term) and columns (one index of sector), at most 2 name sectors of any one owner, and some owner is named exactly 2 times.
All inputs are finite; a program needn't handle non-finite values.
Results may differ from a plain program's by a relative error of at most 0.0037.
Values may be sent and summed in bfloat16 or wider, within the bound.
No kernel may reach another device: no remote copies, remote signals or barrier semaphores. Data moves between devices by JAX's collectives and lax.ppermute only.
A program may use at most 64 MiB of HBM per device.

v0:
```python
import jax
import jax.numpy as jnp
from jax import lax
from jax.sharding import PartitionSpec as P

epsilon = 1e-06


def padded_to(lines, peers):
    spare = -len(lines) % peers
    return jnp.pad(lines, [(0, spare)] + [(0, 0)] * (lines.ndim - 1))


def sum_by_parts(array, axis):
    lines = array.reshape(-1, *array.shape[1:][-1:])
    padded = padded_to(lines, lax.axis_size(axis))
    own = lax.psum_scatter(padded, axis, scatter_dimension=0, tiled=True)
    whole = lax.all_gather(own, axis, axis=0, tiled=True)
    return whole[: len(lines)].reshape(array.shape)


def copy_for_each(array, axis):
    copies = jnp.broadcast_to(array, (lax.axis_size(axis), *array.shape))
    return lax.all_to_all(copies, axis, split_axis=0, concat_axis=0, tiled=True)


def of_everyone(array, axis):
    return copy_for_each(array, axis).sum(axis=0)


def together(arrays, axis):
    line, at, outs = (jnp.concatenate([a.reshape(-1) for a in arrays]), 0, [])
    total = of_everyone(line, axis)
    for a in arrays:
        outs.append(total[at : at + a.size].reshape(a.shape))
        at += a.size
    return tuple(outs)


def cut_along(array, dim, peers):
    before, after = (array.shape[:dim], array.shape[dim + 1 :])
    return jnp.moveaxis(array.reshape(*before, peers, -1, *after), dim, 0)


def sent_and_summed(array, axis, dim):
    tiles = cut_along(array, dim, lax.axis_size(axis))
    arrived = lax.all_to_all(tiles, axis, split_axis=0, concat_axis=0, tiled=True)
    return arrived.astype(jnp.float32).sum(axis=0)


def block_mask(block_size, width):
    positions = jnp.arange(width, dtype=jnp.int32)
    row_keep = positions[None, :] < block_size[:, 0:1]
    column_keep = positions[None, :] < block_size[:, 1:2]
    return row_keep[:, :, None] & column_keep[:, None, :]


def fetch_blocks(masked, source):
    local_count = masked.shape[0]
    width = masked.shape[1]
    bond_count = source.shape[0]
    sector_count = lax.axis_size("sector")
    my_index = lax.axis_index("sector")
    item_count = bond_count * local_count
    flat = masked.reshape(local_count, width * width)
    capacity = max(2, item_count // sector_count + 1)
    per_peer = (
        source.reshape(bond_count, sector_count, local_count)
        .transpose(1, 0, 2)
        .reshape(sector_count, item_count)
    )
    owners = per_peer // local_count
    local_slot = per_peer % local_count
    earlier = jnp.arange(item_count)[None, :] < jnp.arange(item_count)[:, None]
    same_owner = owners[:, :, None] == owners[:, None, :]
    slot_rank = jnp.sum(same_owner & earlier[None, :, :], axis=2)
    from_here = owners == my_index
    slot_numbers = jnp.arange(capacity, dtype=jnp.int32)
    chosen = (
        from_here[:, :, None] & (slot_rank[:, :, None] == slot_numbers[None, None, :])
    ).astype(jnp.float32)
    local_hot = (
        local_slot[:, :, None] == jnp.arange(local_count, dtype=jnp.int32)[None, None, :]
    ).astype(jnp.float32)
    placing = jnp.einsum("pic,pis->pcs", chosen, local_hot).astype(jnp.bfloat16)
    outgoing = jnp.dot(
        placing.reshape(sector_count * capacity, local_count),
        flat,
        preferred_element_type=jnp.float32,
    ).astype(jnp.bfloat16)
    incoming = lax.all_to_all(
        outgoing.reshape(sector_count, capacity, width * width),
        "sector",
        split_axis=0,
        concat_axis=0,
        tiled=True,
    )
    my_owners = lax.dynamic_index_in_dim(owners, my_index, 0, keepdims=False)
    my_ranks = lax.dynamic_index_in_dim(slot_rank, my_index, 0, keepdims=False)
    row_index = my_owners * capacity + my_ranks
    receive_hot = (
        row_index[:, None] == jnp.arange(sector_count * capacity, dtype=jnp.int32)[None, :]
    ).astype(jnp.bfloat16)
    picked = jnp.dot(
        receive_hot,
        incoming.reshape(sector_count * capacity, width * width),
        preferred_element_type=jnp.float32,
    )
    return picked.astype(jnp.bfloat16).reshape(bond_count, local_count, width, width)


def apply_operator(vector, left_env, right_env, source, keep):
    masked = jnp.where(keep, vector, jnp.zeros_like(vector))
    picked = fetch_blocks(masked, source)
    half_product = jnp.einsum(
        "bkij,bkjl->bkil", left_env, picked, preferred_element_type=jnp.float32
    ).astype(jnp.bfloat16)
    bond_terms = jnp.einsum(
        "bkil,bkml->bkim", half_product, right_env, preferred_element_type=jnp.float32
    )
    summed = jnp.sum(bond_terms, axis=0)
    return (jnp.where(keep, summed, jnp.zeros_like(summed)), masked)


def body(wavefunction, left_env, right_env, source, block_size):
    width = wavefunction.shape[1]
    keep = block_mask(block_size, width)
    term_count = lax.axis_size("term")
    term_index = lax.axis_index("term")
    row_count = width // term_count
    total_count = lax.axis_size("sector") * wavefunction.shape[0] * width * width
    partial_value, masked = apply_operator(wavefunction, left_env, right_env, source, keep)
    masked_float = masked.astype(jnp.float32)
    whole_sum = sum_by_parts(partial_value, "term")
    first_product = lax.dynamic_slice_in_dim(whole_sum, term_index * row_count, row_count, 1)
    margin, self_norm = together(
        (jnp.sum(masked_float * whole_sum), jnp.sum(masked_float * masked_float)), "sector"
    )
    residual = whole_sum - margin / self_norm * masked_float
    spread = of_everyone(jnp.sum(residual * residual), "sector")
    next_vector = (residual * lax.rsqrt(spread / total_count + epsilon)).astype(jnp.bfloat16)
    second_partial, _ = apply_operator(next_vector, left_env, right_env, source, keep)
    second_product = sent_and_summed(second_partial.astype(jnp.bfloat16), "term", 1)
    return (first_product, second_product)


def solution(mesh):
    placed = (
        P("sector", None, None),
        P("term", "sector", None, None),
        P("term", "sector", None, None),
        P("term", None),
        P("sector", None),
    )
    return jax.shard_map(
        body,
        mesh=mesh,
        in_specs=placed,
        out_specs=(P("sector", "term", None), P("sector", "term", None)),
        check_vma=False,
    )
```

profile of v0, /device:TPU:1, one launch (start us, length us, event | category | flops | bytes accessed | tf_op | source)
XLA Modules:
  0.0 360.3 jit_solution(6093080198411512897)
XLA Ops:
  7.2 0.0 copy-start
  7.2 0.8 sign_compare_fusion
  8.0 0.7 broadcast_divide_fusion
  8.7 0.8 slice_bitcast_fusion.1
  9.5 0.1 ne.69
  9.6 0.1 copy.89
  9.7 0.1 copy.92
  9.8 0.1 div.38
  9.9 0.1 copy.93
  10.0 0.1 copy.94
  10.1 0.1 rem.43
  10.2 0.1 copy.90
  10.3 0.1 copy.91
  10.4 0.1 copy.96
  10.5 0.5 convert_reduce_fusion.1
  10.9 0.1 copy.97
  11.0 0.1 iota_compare_fusion.6
  11.1 1.5 fusion.45
  12.6 0.5 copy.125
  13.0 0.1 convolution_convert_fusion.4
  13.2 3.2 convolution_convert_fusion.1
  16.3 5.9 %reshape.193 = bf16[16,2,65536]{2,1,0:T(2,128)(2,1)} reshape(bf16[32,65536]{1,0:T(8,128)(2,1)} %convolution_convert_fusion.1) | data formatting | bytes 8388608 | tf_op jit(solution)/shard_map/reshape | solution.py:92
  22.2 7.6 %all-to-all-start = ((bf16[16,2,65536]{2,1,0:T(2,128)(2,1)}), bf16[16,2,65536]{2,1,0:T(2,128)(2,1)}, u32[]{:S(2)}, u32[]{:S(2)}) async-start(bf16[16,2,65536]{2,1,0:T(2,128)(2,1)} %reshape.193), calls=%async_computation | async-start | bytes 8388608 | tf_op jit(solution)/shard_map/all_to_all | solution.py:91
  29.8 0.0 reduce-scatter.2.cloned.1.call-start
  29.9 62.4 %all-to-all-done = bf16[16,2,65536]{2,1,0:T(2,128)(2,1)} async-done(((bf16[16,2,65536]{2,1,0:T(2,128)(2,1)}), bf16[16,2,65536]{2,1,0:T(2,128)(2,1)}, u32[]{:S(2)}, u32[]{:S(2)}) %all-to-all-start) | async-done | bytes 4194336 | tf_op jit(solution)/shard_map/all_to_all | solution.py:91
  92.3 5.4 %reshape.194 = bf16[32,65536]{1,0:T(8,128)(2,1)} reshape(bf16[16,2,65536]{2,1,0:T(2,128)(2,1)} %all-to-all-done) | data formatting | bytes 8388608 | tf_op jit(solution)/shard_map/reshape | solution.py:106
  97.7 3.2 convolution_convert_fusion.3
  100.9 0.7 copy.126
  101.7 1.6 slice.19
  103.3 0.0 copy-done
  103.3 0.0 copy-start.1
  103.3 5.1 %and_select_fusion.2 = f32[6,256,256]{2,1,0:T(8,128)} fusion(bf16[3,6,256,256]{3,2,1,0:T(8,128)(2,1)S(1)} %copy-done, bf16[3,6,256,256]{3,2,1,0:T(8,128)(2,1)} %bitcast.73, bf16[3,6,256,256]{3,2,1,0:T(8,128)(2,1)} %param.6, pred[6,256]{1,0:T(8,128)(4,1)S(1)} %get-tuple-element.12, pred[6,256]{1,0:T(8,128)(4,1)S(1)} %get-tuple-element.13), kind=kOutput, calls=%fused_computation.6 | convolution fusion | flops 1209925632 | bytes 8653824 | tf_op jit(solution)/shard_map/bkil,bkml->bkim/dot_general | solution.py:118
  108.4 0.0 reduce-scatter.2.cloned.1.call-update
  108.5 0.0 all-gather.2.cloned.1.call-start
  108.5 58.0 %reduce-scatter.2.cloned.1.call-done = f32[96,256]{1,0:T(8,128)} async-done(((f32[1536,256]{1,0:T(8,128)}), f32[96,256]{1,0:T(8,128)}) %reduce-scatter.2.cloned.1.call-update) | async-done | bytes 98320 | tf_op jit(solution)/shard_map/reduce_scatter | solution.py:17
  166.5 0.0 all-gather.2.cloned.1.call-update
  166.5 42.5 %all-gather.2.cloned.1.call-done = f32[1536,256]{1,0:T(8,128)} async-done(((f32[96,256]{1,0:T(8,128)}), f32[1536,256]{1,0:T(8,128)}) %all-gather.2.cloned.1.call-update) | async-done | bytes 1572880 | tf_op jit(solution)/shard_map/all_gather | solution.py:18
  209.1 0.0 copy-done.1
  209.1 2.6 fusion.24
  211.7 1.4 pad_maximum_fusion
  213.1 12.8 %all_to_all.27 = f32[16,1,2]{2,1,0:T(1,128)S(1)} all-to-all(f32[16,1,2]{2,1,0:T(1,128)S(1)} %broadcast_in_dim.4), channel_id=1, replica_groups=mesh['term'=16,'sector'=16] {'sector'}, dimensions={0} | all-to-all | bytes 256 | tf_op jit(solution)/shard_map/all_to_all | solution.py:24
  226.0 0.6 fusion.55
  227.9 2.6 multiply_reduce_fusion
  230.5 0.6 broadcast_in_dim.5
  231.2 9.1 %all_to_all.28 = f32[16,1,1]{2,1,0:T(1,128)S(1)} all-to-all(f32[16,1,1]{2,1,0:T(1,128)S(1)} %broadcast_in_dim.5), channel_id=1, replica_groups=mesh['term'=16,'sector'=16] {'sector'}, dimensions={0} | all-to-all | bytes 128 | tf_op jit(solution)/shard_map/all_to_all | solution.py:24
  240.3 0.6 reduce_sum.80
  241.6 1.9 fusion.44
  243.6 0.5 copy.127
  244.0 3.2 convolution_convert_fusion
  247.2 5.9 %reshape.201 = bf16[16,2,65536]{2,1,0:T(2,128)(2,1)} reshape(bf16[32,65536]{1,0:T(8,128)(2,1)} %convolution_convert_fusion) | data formatting | bytes 8388608 | tf_op jit(solution)/shard_map/reshape | solution.py:92
  253.1 52.4 %all_to_all.29 = bf16[16,2,65536]{2,1,0:T(2,128)(2,1)} all-to-all(bf16[16,2,65536]{2,1,0:T(2,128)(2,1)} %reshape.201), channel_id=1, replica_groups=mesh['term'=16,'sector'=16] {'sector'}, dimensions={0} | all-to-all | bytes 8388608 | tf_op jit(solution)/shard_map/all_to_all | solution.py:91
  305.5 5.4 %reshape.202 = bf16[32,65536]{1,0:T(8,128)(2,1)} reshape(bf16[16,2,65536]{2,1,0:T(2,128)(2,1)} %all_to_all.29) | data formatting | bytes 8388608 | tf_op jit(solution)/shard_map/reshape | solution.py:106
  310.9 3.2 convolution_convert_fusion.2
  314.2 0.7 copy.128
  314.9 1.6 slice.20
  316.5 3.9 %fusion.27 = bf16[6,256,256]{2,1,0:T(8,128)(2,1)S(1)} fusion(bf16[3,6,256,256]{3,2,1,0:T(8,128)(2,1)S(1)} %copy-done, bf16[3,6,256,256]{3,2,1,0:T(8,128)(2,1)} %bitcast.72, bf16[3,6,256,256]{3,2,1,0:T(8,128)(2,1)} %param.6, pred[6,256]{1,0:T(8,128)(4,1)S(1)} %get-tuple-element.12, pred[6,256]{1,0:T(8,128)(4,1)S(1)} %get-tuple-element.13), kind=kOutput, calls=%fused_computation.28 | convolution fusion | flops 1210318848 | bytes 7867392 | tf_op jit(solution)/shard_map/bkil,bkml->bkim/dot_general | solution.py:118
  320.4 1.0 copy.164
  321.4 8.6 %all-to-all-start.4 = ((bf16[16,6,16,256]{3,2,1,0:T(8,128)(2,1)}), bf16[16,6,16,256]{3,2,1,0:T(8,128)(2,1)S(1)}, u32[]{:S(2)}, u32[]{:S(2)}) async-start(bf16[16,6,16,256]{3,2,1,0:T(8,128)(2,1)} %bitcast.71), calls=%async_computation.5 | async-start | bytes 1572864 | tf_op jit(solution)/shard_map/all_to_all | solution.py:47
  330.0 1.5 constant_dynamic-slice_fusion
  331.5 21.2 %all-to-all-done.4 = bf16[16,6,16,256]{3,2,1,0:T(8,128)(2,1)S(1)} async-done(((bf16[16,6,16,256]{3,2,1,0:T(8,128)(2,1)}), bf16[16,6,16,256]{3,2,1,0:T(8,128)(2,1)S(1)}, u32[]{:S(2)}, u32[]{:S(2)}) %all-to-all-start.4) | async-done | bytes 786464 | tf_op jit(solution)/shard_map/all_to_all | solution.py:47
  352.7 0.8 convert_reduce_fusion
  (9 shorter events, 0.1 us)
Async XLA Ops:
  7.2 96.1 %copy-start = (bf16[3,6,256,256]{3,2,1,0:T(8,128)(2,1)S(1)}, bf16[3,6,256,256]{3,2,1,0:T(8,128)(2,1)}, u32[]{:S(2)}) copy-start(bf16[3,6,256,256]{3,2,1,0:T(8,128)(2,1)} %param.7) | copy-start | bytes 7077892
  22.2 70.1 %all-to-all-start = ((bf16[16,2,65536]{2,1,0:T(2,128)(2,1)}), bf16[16,2,65536]{2,1,0:T(2,128)(2,1)}, u32[]{:S(2)}, u32[]{:S(2)}) async-start(bf16[16,2,65536]{2,1,0:T(2,128)(2,1)} %reshape.193), calls=%async_computation | async-start | bytes 8388608 | tf_op jit(solution)/shard_map/all_to_all | solution.py:91
  29.8 136.7 %reduce-scatter.2.cloned.1.call-start = ((), (), s32[]{:S(2)}) async-start(), calls=%async_computation.6 | async-start | bytes 1671168 | tf_op jit(solution)/shard_map/reduce_scatter | solution.py:17
  103.3 105.8 %copy-start.1 = (bf16[6,256,256]{2,1,0:T(8,128)(2,1)S(1)}, bf16[6,256,256]{2,1,0:T(8,128)(2,1)}, u32[]{:S(2)}) copy-start(bf16[6,256,256]{2,1,0:T(8,128)(2,1)} %param.5) | copy-start | bytes 2359300
  108.5 100.6 %all-gather.2.cloned.1.call-start = ((), (), s32[]{:S(2)}) async-start(), calls=%async_computation.7 | async-start | bytes 1671168 | tf_op jit(solution)/shard_map/all_gather | solution.py:18
  321.4 31.3 %all-to-all-start.4 = ((bf16[16,6,16,256]{3,2,1,0:T(8,128)(2,1)}), bf16[16,6,16,256]{3,2,1,0:T(8,128)(2,1)S(1)}, u32[]{:S(2)}, u32[]{:S(2)}) async-start(bf16[16,6,16,256]{3,2,1,0:T(8,128)(2,1)} %bitcast.71), calls=%async_computation.5 | async-start | bytes 1572864 | tf_op jit(solution)/shard_map/all_to_all | solution.py:47
Sparse Core Ops, SparseCore 0:
  108.6 57.8 reduce-scatter.1
  168.3 40.6 all-gather.1
where the time goes:
time: 361 us; the launch traced here: 360 us
  waiting for transfers between devices  184 us (51%)
  blocking collectives  74.4 us (21%)
  local copies, waits for them, and re-layouts  33.7 us (9%)
  matrix products  22 us (6%)
  starting transfers between devices  16.3 us (5%)
  between operations  16.2 us (4%)
  other arithmetic  13.5 us (4%)
    all_to_all x1, waiting for transfers between devices, fetch_blocks(): lax.all_to_all(outgoing.reshape(sector_count, capacity, width * width), '...  62.4 us
    reduce_scatter x1, waiting for transfers between devices, sum_by_parts(): own = lax.psum_scatter(padded, axis, scatter_dimension=0, tiled=True)  58 us
    all_to_all x1, blocking collectives, fetch_blocks(): lax.all_to_all(outgoing.reshape(sector_count, capacity, width * width), '...  52.4 us
    all_gather x1, waiting for transfers between devices, sum_by_parts(): whole = lax.all_gather(own, axis, axis=0, tiled=True)  42.5 us
    all_to_all x2, blocking collectives, copy_for_each(): return lax.all_to_all(copies, axis, split_axis=0, concat_axis=0, tiled=True)  22 us
    all_to_all x1, waiting for transfers between devices, sent_and_summed(): lax.all_to_all(tiles, axis, split_axis=0, concat_axis=0, tiled=True)  21.2 us
    reshape x2, local copies, waits for them, and re-layouts, fetch_blocks(): outgoing.reshape(sector_count, capacity, width * width)  11.7 us
    reshape x2, local copies, waits for them, and re-layouts, fetch_blocks(): incoming.reshape(sector_count * capacity, width * width)  10.8 us
  transfers between devices with their start and end apart: 4, of which 4 were waited for; matrix products, arithmetic and copies ran while one was open for 0% of the time, Pallas kernels for 0%

commit v1 on v0

v1 whole, which is shorter than its diff:
```python
import functools

import jax
import jax.numpy as jnp
from jax import lax
from jax.experimental import pallas as pl
from jax.experimental.pallas import tpu as pltpu
from jax.sharding import PartitionSpec as P

epsilon = 1e-06
EXTRA = 16
F32 = jnp.float32
BF16 = jnp.bfloat16


def pieces_of(value):
    high = value.astype(BF16)
    rest = value - high.astype(F32)
    middle = rest.astype(BF16)
    low = (rest - middle.astype(F32)).astype(BF16)
    return [high, middle, low]


def joined(parts, at):
    return parts[:, at] + parts[:, at + 1] + parts[:, at + 2]


def ratio(above, below):
    live = below > 0
    return jnp.where(live, above / jnp.where(live, below, 1.0), 0.0)


def totals_of(extra):
    parts = extra.astype(F32)
    norms, margins, spreads = joined(parts, 0), joined(parts, 3), joined(parts, 6)
    norm = jnp.sum(norms, axis=0, keepdims=True)
    margin = jnp.sum(margins, axis=0, keepdims=True)
    own = ratio(margins, norms)
    shift = ratio(margin, norm) - own
    moved = spreads - 2.0 * shift * (margins - own * norms) + shift * shift * norms
    return norm, margin, jnp.sum(moved, axis=0, keepdims=True)


def rows_of_pieces(values, width):
    rows = [row for value in values for row in pieces_of(value)]
    rows = [jnp.broadcast_to(row, (1, width)).astype(F32) for row in rows]
    rows.append(jnp.zeros((EXTRA - len(rows), width), F32))
    return jnp.concatenate(rows, axis=0).astype(BF16)


def keep_of(rows, columns, shape, first_row=0):
    row = lax.broadcasted_iota(jnp.int32, shape, 0) + first_row
    column = lax.broadcasted_iota(jnp.int32, shape, 1)
    return (row < rows) & (column < columns)


def pack_masked_kernel(slots, sizes, wave, out, masked):
    peer = pl.program_id(0)
    count, width = wave.shape[0], wave.shape[1]

    @pl.when(peer == 0)
    def _():
        for k in range(count):
            keep = keep_of(sizes[2 * k], sizes[2 * k + 1], (width, width))
            masked[k] = jnp.where(keep, wave[k].astype(F32), 0.0).astype(BF16)

    capacity = out.shape[1] // width
    for c in range(capacity):
        out[0, pl.ds(c * width, width), :] = masked[slots[peer * capacity + c]]


def pack_masked(slots, sizes, wave, peers, capacity):
    count, width, _ = wave.shape
    return pl.pallas_call(
        pack_masked_kernel,
        grid_spec=pltpu.PrefetchScalarGridSpec(
            num_scalar_prefetch=2,
            grid=(peers,),
            in_specs=[pl.BlockSpec((count, width, width), lambda p, *_: (0, 0, 0))],
            out_specs=pl.BlockSpec((1, capacity * width, width), lambda p, *_: (p, 0, 0)),
            scratch_shapes=[pltpu.VMEM((count, width, width), BF16)],
        ),
        out_shape=jax.ShapeDtypeStruct((peers, capacity * width, width), BF16),
        name="pack_masked",
    )(slots, sizes, wave)


def pack_first_kernel(slots, gathered, out):
    peer = pl.program_id(0)
    terms, lines, width = gathered.shape
    rows = width // terms
    capacity = (out.shape[1] - EXTRA) // width
    for c in range(capacity):
        slot = slots[peer * capacity + c]
        start = pl.multiple_of(slot * rows, rows)
        block = gathered[:, pl.ds(start, rows), :]
        out[0, pl.ds(c * width, width), :] = block.reshape(width, width)
    norm, margin, spread = totals_of(gathered[:, pl.ds(lines - EXTRA, EXTRA), :])
    out[0, pl.ds(capacity * width, EXTRA), :] = rows_of_pieces((norm, margin, spread), width)


def pack_first(slots, gathered, peers, capacity):
    terms, lines, width = gathered.shape
    out_lines = capacity * width + EXTRA
    return pl.pallas_call(
        pack_first_kernel,
        grid_spec=pltpu.PrefetchScalarGridSpec(
            num_scalar_prefetch=1,
            grid=(peers,),
            in_specs=[pl.BlockSpec((terms, lines, width), lambda p, *_: (0, 0, 0))],
            out_specs=pl.BlockSpec((1, out_lines, width), lambda p, *_: (p, 0, 0)),
        ),
        out_shape=jax.ShapeDtypeStruct((peers, out_lines, width), BF16),
        name="pack_first",
    )(slots, gathered)


def bond_sum(vectors, left, right):
    total = None
    for b, vector in enumerate(vectors):
        half = jnp.dot(left[b, 0], vector, preferred_element_type=F32).astype(BF16)
        term = lax.dot_general(half, right[b, 0], (((1,), (1,)), ((), ())), preferred_element_type=F32)
        total = term if total is None else total + term
    return total


def store_partial(total, sizes, out):
    k = pl.program_id(0)
    keep = keep_of(sizes[2 * k], sizes[2 * k + 1], total.shape)
    total = jnp.where(keep, total, 0.0).astype(BF16)
    out[:, 0] = total.reshape(out.shape[0], out.shape[2], out.shape[3])


def first_kernel(bonds, owners, ranks, sizes, *refs):
    left, right, out = refs[bonds:]
    store_partial(bond_sum([r[0] for r in refs[:bonds]], left, right), sizes, out)


def second_kernel(bonds, count, owners, ranks, sizes, *refs):
    waves, firsts = refs[:bonds], refs[bonds : 2 * bonds]
    extra, left, right, out = refs[2 * bonds :]
    norm, margin, spread = totals_of(extra[...])
    scale = lax.rsqrt(jnp.maximum(spread, 0.0) / count + epsilon)
    share = margin / norm
    vectors = []
    for wave, first in zip(waves, firsts):
        residual = first[0].astype(F32) - share * wave[0].astype(F32)
        vectors.append((residual * scale).astype(BF16))
    store_partial(bond_sum(vectors, left, right), sizes, out)


def product(owners, ranks, sizes, arrived, left, right, terms, total_count=None):
    bonds, count, width, _ = left.shape

    def picked(b):
        return pl.BlockSpec((1, width, width), lambda k, own, rank, *_: (own[b * count + k], rank[b * count + k], 0))

    env = pl.BlockSpec((bonds, 1, width, width), lambda k, *_: (0, k, 0, 0))
    operands, specs = [], []
    for array in arrived:
        operands += [array] * bonds
        specs += [picked(b) for b in range(bonds)]
    if total_count is None:
        kernel = functools.partial(first_kernel, bonds)
    else:
        kernel = functools.partial(second_kernel, bonds, total_count)
        lines = arrived[1].shape[1]
        operands.append(arrived[1])
        specs.append(pl.BlockSpec((arrived[1].shape[0], EXTRA, width), lambda k, *_: (0, lines // EXTRA - 1, 0)))
    return pl.pallas_call(
        kernel,
        grid_spec=pltpu.PrefetchScalarGridSpec(
            num_scalar_prefetch=3,
            grid=(count,),
            in_specs=specs + [env, env],
            out_specs=pl.BlockSpec((terms, 1, width // terms, width), lambda k, *_: (0, k, 0, 0)),
        ),
        out_shape=jax.ShapeDtypeStruct((terms, count, width // terms, width), BF16),
        name="product",
    )(owners, ranks, sizes, *operands, left, right)


def middle_kernel(term, sizes, arrived, wave, first_out, message):
    terms, count, rows, width = arrived.shape
    summed = arrived[0].astype(F32)
    for t in range(1, terms):
        summed = summed + arrived[t].astype(F32)
    first_out[...] = summed
    kept = []
    for k in range(count):
        keep = keep_of(sizes[2 * k], sizes[2 * k + 1], (rows, width), term[0] * rows)
        kept.append(jnp.where(keep, wave[k].astype(F32), 0.0)[None])
    masked = jnp.concatenate(kept, axis=0)

    def whole(values):
        return jnp.sum(jnp.sum(jnp.sum(values, axis=0), axis=0, keepdims=True), axis=1, keepdims=True)

    margin = whole(masked * summed)
    norm = whole(masked * masked)
    residual = summed - ratio(margin, norm)[None] * masked
    spread = whole(residual * residual)
    extra = rows_of_pieces((norm, margin, spread), width)
    lines = summed.astype(BF16).reshape(count * rows, width)
    for t in range(terms):
        message[t, pl.ds(0, count * rows), :] = lines
        message[t, pl.ds(count * rows, EXTRA), :] = extra


def middle(term, sizes, arrived, wave):
    terms, count, rows, width = arrived.shape
    lines = count * rows + EXTRA
    return pl.pallas_call(
        middle_kernel,
        grid_spec=pltpu.PrefetchScalarGridSpec(
            num_scalar_prefetch=2,
            grid=(1,),
            in_specs=[
                pl.BlockSpec((terms, count, rows, width), lambda i, *_: (0, 0, 0, 0)),
                pl.BlockSpec((count, rows, width), lambda i, t, *_: (0, t[0], 0)),
            ],
            out_specs=[
                pl.BlockSpec((count, rows, width), lambda i, *_: (0, 0, 0)),
                pl.BlockSpec((terms, lines, width), lambda i, *_: (0, 0, 0)),
            ],
        ),
        out_shape=[
            jax.ShapeDtypeStruct((count, rows, width), F32),
            jax.ShapeDtypeStruct((terms, lines, width), BF16),
        ],
        name="middle",
    )(term, sizes, arrived, wave)


def exchanged(array, axis):
    return lax.all_to_all(array, axis, split_axis=0, concat_axis=0, tiled=True)


def routes(source, count, capacity):
    peers = lax.axis_size("sector")
    me = lax.axis_index("sector")
    bonds = source.shape[0]
    needs = source.reshape(bonds, peers, count).transpose(1, 0, 2).reshape(peers, bonds * count)
    first_mine = me * count
    local = needs - first_mine
    here = (local >= 0) & (local < count)
    items = bonds * count
    earlier = jnp.arange(items)[:, None] < jnp.arange(items)[None, :]
    rank = jnp.sum(here[:, :, None] & earlier[None], axis=1)
    chosen = here[:, None, :] & (rank[:, None, :] == jnp.arange(capacity)[None, :, None])
    slots = jnp.sum(jnp.where(chosen, local[:, None, :], 0), axis=2).reshape(-1)
    mine = lax.dynamic_index_in_dim(needs, me, 0, keepdims=False)
    owners = lax.div(mine, jnp.int32(count))
    ranks = jnp.sum((owners[:, None] == owners[None, :]) & earlier, axis=0)
    return slots.astype(jnp.int32), owners, ranks.astype(jnp.int32)


def body(wavefunction, left_env, right_env, source, block_size):
    count, width, _ = wavefunction.shape
    peers, terms = lax.axis_size("sector"), lax.axis_size("term")
    capacity = max(2, left_env.shape[0] * count // peers + 1)
    term = lax.axis_index("term").reshape(1).astype(jnp.int32)
    sizes = block_size.reshape(-1)
    slots, owners, ranks = routes(source, count, capacity)
    waves = exchanged(pack_masked(slots, sizes, wavefunction, peers, capacity), "sector")
    partial = product(owners, ranks, sizes, [waves], left_env, right_env, terms)
    first_product, message = middle(term, sizes, exchanged(partial, "term"), wavefunction)
    gathered = exchanged(message, "term")
    firsts = exchanged(pack_first(slots, gathered, peers, capacity), "sector")
    total_count = peers * count * width * width
    partial = product(owners, ranks, sizes, [waves, firsts], left_env, right_env, terms, total_count)
    second_product = jnp.sum(exchanged(partial, "term").astype(F32), axis=0)
    return (first_product, second_product)


def solution(mesh):
    placed = (
        P("sector", None, None),
        P("term", "sector", None, None),
        P("term", "sector", None, None),
        P("term", None),
        P("sector", None),
    )
    return jax.shard_map(
        body,
        mesh=mesh,
        in_specs=placed,
        out_specs=(P("sector", "term", None), P("sector", "term", None)),
        check_vma=False,
    )
```

time: 361 us -> 261 us (0.72)
  waiting for transfers between devices: 184 us -> 84.3 us
  blocking collectives: 74.4 us -> 115 us
  Pallas kernels: 0 us -> 36.8 us
  local copies, waits for them, and re-layouts: 33.7 us -> 4.06 us
  matrix products: 22 us -> 0 us
  between operations: 16.2 us -> 0.68 us
  other arithmetic: 13.5 us -> 1.86 us
    reduce_scatter x1 -> x0, waiting for transfers between devices: 58 us -> none  [sum_by_parts(): own = lax.psum_scatter(padded, axis, scatter_dimension=0, tiled=True)]
    all_gather x1 -> x0, waiting for transfers between devices: 42.5 us -> none  [sum_by_parts(): whole = lax.all_gather(own, axis, axis=0, tiled=True)]
    all_to_all x3, blocking collectives: 74.4 us -> 115 us  [exchanged(): return lax.all_to_all(array, axis, split_axis=0, concat_axis=0, tiled=True)]
    pallas_call x0 -> x5, Pallas kernels: none -> 36.8 us  [the longest x2 16.8 us: product(): pl.pallas_call(kernel, grid_spec=pltpu.PrefetchScalarGridSpec(num_scalar_...]
    dot_general x7 -> x0, matrix products: 22 us -> none  [the longest x2 9.06 us: apply_operator(): jnp.einsum('bkil,bkml->bkim', half_product, right_env, preferred_element_...]
    reshape x5 -> x4, local copies, waits for them, and re-layouts: 23.5 us -> 2.06 us  [the longest x2 0.77 us: routes(): source.reshape(bonds, peers, count).transpose(1, 0, 2)]
    reduce_sum x6 -> x4, other arithmetic: 7.13 us -> 1.65 us  [the longest x1 0.75 us: body(): second_product = jnp.sum(exchanged(partial, 'term').astype(F32), axis=0)]
    unnamed x10 -> x5, local copies, waits for them, and re-layouts: 5.62 us -> 1.65 us
  transfers between devices with their start and end apart: 4 -> 2, of which waited for: 4 -> 2; matrix products, arithmetic and copies ran while one was open for 0% -> 0% of each run, Pallas kernels for 0% -> 0%
where the time goes in v1:
time: 261 us; the launch traced here: 260 us
  blocking collectives  115 us (44%)
  waiting for transfers between devices  84.3 us (32%)
  Pallas kernels  36.8 us (14%)
  starting transfers between devices  17.9 us (7%)
  local copies, waits for them, and re-layouts  4.06 us (2%)
    all_to_all x3, blocking collectives, exchanged(): return lax.all_to_all(array, axis, split_axis=0, concat_axis=0, tiled=True)  115 us
    all_to_all x2, waiting for transfers between devices, exchanged(): return lax.all_to_all(array, axis, split_axis=0, concat_axis=0, tiled=True)  84.3 us
    all_to_all x2, starting transfers between devices, exchanged(): return lax.all_to_all(array, axis, split_axis=0, concat_axis=0, tiled=True)  17.9 us
    pallas_call x2, Pallas kernels, product(): pl.pallas_call(kernel, grid_spec=pltpu.PrefetchScalarGridSpec(num_scalar_...  16.8 us
    pallas_call x1, Pallas kernels, pack_first(): pl.pallas_call(pack_first_kernel, grid_spec=pltpu.PrefetchScalarGridSpec(...  8.99 us
    pallas_call x1, Pallas kernels, pack_masked(): pl.pallas_call(pack_masked_kernel, grid_spec=pltpu.PrefetchScalarGridSpec...  7.94 us
  transfers between devices with their start and end apart: 2, of which 2 were waited for; matrix products, arithmetic and copies ran while one was open for 0% of the time, Pallas kernels for 0%

profile of v1, /device:TPU:1, one launch (start us, length us, event | category | flops | bytes accessed | tf_op | source)
XLA Modules:
  0.0 260.2 jit_solution(16484986904441537574)
XLA Ops:
  0.6 0.8 copy.19
  1.4 0.7 reshape.59.sizes
  2.1 0.8 reshape.60
  2.9 0.1 copy.20
  3.0 0.1 copy.22
  3.0 0.1 copy.21
  3.1 0.1 convert_reduce_fusion.1
  3.3 0.1 select_reduce_fusion
  3.4 0.1 copy.23
  3.5 0.6 reshape.62.slots
  4.1 7.9 %pack_masked.1 = bf16[16,512,256]{2,1,0:T(8,128)(2,1)} custom-call(s32[32]{0:T(128)} %reshape.62.slots, s32[12]{0:T(128)} %reshape.59.sizes, bf16[6,256,256]{2,1,0:T(8,128)(2,1)} %wave.3), custom_call_target="tpu_custom_call" | custom-call | tf_op jit(solution)/shard_map/pack_masked/pallas_call | solution.py:74
  12.0 7.6 %all-to-all-start = ((bf16[16,512,256]{2,1,0:T(8,128)(2,1)}), bf16[16,512,256]{2,1,0:T(8,128)(2,1)}, u32[]{:S(2)}, u32[]{:S(2)}) async-start(bf16[16,512,256]{2,1,0:T(8,128)(2,1)} %pack_masked.1), calls=%async_computation | async-start | bytes 8388608 | tf_op jit(solution)/shard_map/all_to_all | solution.py:235
  19.6 0.2 fusion.1.owners
  19.8 0.0 copy-start.1
  19.8 0.7 convert_reduce_fusion.2.ranks
  20.5 61.6 %all-to-all-done.refs_0_.refs_1_.refs_2_ = bf16[16,512,256]{2,1,0:T(8,128)(2,1)} async-done(((bf16[16,512,256]{2,1,0:T(8,128)(2,1)}), bf16[16,512,256]{2,1,0:T(8,128)(2,1)}, u32[]{:S(2)}, u32[]{:S(2)}) %all-to-all-start) | async-done | bytes 4194336 | tf_op jit(solution)/shard_map/all_to_all | solution.py:235
  82.1 0.0 copy-done.1
  82.1 7.8 %product.2 = bf16[16,6,16,256]{3,2,1,0:T(8,128)(2,1)} custom-call(s32[18]{0:T(128)} %copy-done.1, s32[18]{0:T(128)} %convert_reduce_fusion.2.ranks, s32[12]{0:T(128)} %reshape.59.sizes, bf16[16,512,256]{2,1,0:T(8,128)(2,1)} %all-to-all-done.refs_0_.refs_1_.refs_2_, bf16[16,512,256]{2,1,0:T(8,128)(2,1)} %all-to-all-done.refs_0_.refs_1_.refs_2_, ...), custom_call_target="tpu_custom_call" | custom-call | tf_op jit(solution)/shard_map/product/pallas_call | solution.py:170
  89.9 10.3 %all-to-all-start.1 = ((bf16[16,6,16,256]{3,2,1,0:T(8,128)(2,1)}), bf16[16,6,16,256]{3,2,1,0:T(8,128)(2,1)S(1)}, u32[]{:S(2)}, u32[]{:S(2)}) async-start(bf16[16,6,16,256]{3,2,1,0:T(8,128)(2,1)} %product.2), calls=%async_computation.1 | async-start | bytes 1572864 | tf_op jit(solution)/shard_map/all_to_all | solution.py:235
  100.2 22.7 %all-to-all-done.1.arrived = bf16[16,6,16,256]{3,2,1,0:T(8,128)(2,1)S(1)} async-done(((bf16[16,6,16,256]{3,2,1,0:T(8,128)(2,1)}), bf16[16,6,16,256]{3,2,1,0:T(8,128)(2,1)S(1)}, u32[]{:S(2)}, u32[]{:S(2)}) %all-to-all-start.1) | async-done | bytes 786464 | tf_op jit(solution)/shard_map/all_to_all | solution.py:235
  122.9 0.0 copy-start
  122.9 0.9 copy-done
  123.8 3.1 %middle.1 = (f32[6,16,256]{2,1,0:T(8,128)}, bf16[16,112,256]{2,1,0:T(8,128)(2,1)}) custom-call(s32[1]{0:T(128)} %bitcast.term, s32[12]{0:T(128)} %reshape.59.sizes, bf16[16,6,16,256]{3,2,1,0:T(8,128)(2,1)} %copy-done, bf16[6,256,256]{2,1,0:T(8,128)(2,1)} %wave.3), custom_call_target="tpu_custom_call" | custom-call | tf_op jit(solution)/shard_map/middle/pallas_call | solution.py:212
  126.9 28.9 %all_to_all.25.gathered = bf16[16,112,256]{2,1,0:T(8,128)(2,1)} all-to-all(bf16[16,112,256]{2,1,0:T(8,128)(2,1)} %get-tuple-element.5), channel_id=1, replica_groups=mesh['term'=16,'sector'=16] {'term'}, dimensions={0} | all-to-all | bytes 1835008 | tf_op jit(solution)/shard_map/all_to_all | solution.py:235
  155.8 9.0 %pack_first.1 = bf16[16,528,256]{2,1,0:T(8,128)(2,1)} custom-call(s32[32]{0:T(128)} %reshape.62.slots, bf16[16,112,256]{2,1,0:T(8,128)(2,1)} %all_to_all.25.gathered), custom_call_target="tpu_custom_call" | custom-call | tf_op jit(solution)/shard_map/pack_first/pallas_call | solution.py:105
  164.8 58.8 %all_to_all.26.refs_3_.refs_4_.refs_5_.refs_6_ = bf16[16,528,256]{2,1,0:T(8,128)(2,1)} all-to-all(bf16[16,528,256]{2,1,0:T(8,128)(2,1)} %pack_first.1), channel_id=1, replica_groups=mesh['term'=16,'sector'=16] {'sector'}, dimensions={0} | all-to-all | bytes 8650752 | tf_op jit(solution)/shard_map/all_to_all | solution.py:235
  223.5 9.0 %product.3 = bf16[16,6,16,256]{3,2,1,0:T(8,128)(2,1)} custom-call(s32[18]{0:T(128)} %copy-done.1, s32[18]{0:T(128)} %convert_reduce_fusion.2.ranks, s32[12]{0:T(128)} %reshape.59.sizes, bf16[16,512,256]{2,1,0:T(8,128)(2,1)} %all-to-all-done.refs_0_.refs_1_.refs_2_, bf16[16,512,256]{2,1,0:T(8,128)(2,1)} %all-to-all-done.refs_0_.refs_1_.refs_2_, ...), custom_call_target="tpu_custom_call" | custom-call | tf_op jit(solution)/shard_map/product/pallas_call | solution.py:170
  232.5 26.9 %all_to_all.27 = bf16[16,6,16,256]{3,2,1,0:T(8,128)(2,1)S(1)} all-to-all(bf16[16,6,16,256]{3,2,1,0:T(8,128)(2,1)} %product.3), channel_id=1, replica_groups=mesh['term'=16,'sector'=16] {'term'}, dimensions={0} | all-to-all | bytes 1572864 | tf_op jit(solution)/shard_map/all_to_all | solution.py:235
  259.4 0.8 convert_reduce_fusion
  (3 shorter events, 0.0 us)
Async XLA Ops:
  12.0 70.1 %all-to-all-start = ((bf16[16,512,256]{2,1,0:T(8,128)(2,1)}), bf16[16,512,256]{2,1,0:T(8,128)(2,1)}, u32[]{:S(2)}, u32[]{:S(2)}) async-start(bf16[16,512,256]{2,1,0:T(8,128)(2,1)} %pack_masked.1), calls=%async_computation | async-start | bytes 8388608 | tf_op jit(solution)/shard_map/all_to_all | solution.py:235
  19.8 62.3 %copy-start.1 = (s32[18]{0:T(128)}, s32[18]{0:T(128)S(1)}, u32[]{:S(2)}) copy-start(s32[18]{0:T(128)S(1)} %fusion.1.owners) | copy-start | bytes 220
  89.9 33.0 %all-to-all-start.1 = ((bf16[16,6,16,256]{3,2,1,0:T(8,128)(2,1)}), bf16[16,6,16,256]{3,2,1,0:T(8,128)(2,1)S(1)}, u32[]{:S(2)}, u32[]{:S(2)}) async-start(bf16[16,6,16,256]{3,2,1,0:T(8,128)(2,1)} %product.2), calls=%async_computation.1 | async-start | bytes 1572864 | tf_op jit(solution)/shard_map/all_to_all | solution.py:235
  122.9 0.9 copy-start
